TPU v7x, 32 devices: a whole 2x2x4 slice. The times are simulated.
32 devices in a mesh: lat: 16 (over z, x, core), tm: 2 (over y).
Axes of the slice: x: 2, y: 2, z: 4, core: 2. Of those that a mesh axis runs over, the one named last changes fastest.
Arguments:
- fields: bfloat16 [512, 64, 1024], P('lat', 'tm'), may hold values from -16 to 16
Outputs:
- covariance: float32 [64, 64], P('tm')
All inputs are finite; a program needn't handle non-finite values.
Results may differ from a plain program's by a relative error of at most 0.0003.
Values may be sent and summed in bfloat16 or wider, within the bound.
A program may use at most 64 MiB of HBM per device.

v0:
```python
import math

import jax
import jax.numpy as jnp
from jax import lax
from jax.sharding import PartitionSpec as P

TRUNC = 341
MSLOT = 384
DSLOT = 384


def start_value(order, sine_lat):
    log_start = 0.5 * (
        math.log(0.5)
        + lax.lgamma(order + 1.5)
        - (0.5 * math.log(math.pi) - math.log(2.0))
        - lax.lgamma(order + 1.0)
    ) + order * jnp.log(sine_lat)
    taper = jnp.clip((log_start + 70.0) / 10.0, 0.0, 1.0)
    return jnp.exp(jnp.maximum(log_start, -80.0)) * taper


def step_factors(order, degree):
    top = jnp.sqrt((4.0 * degree * degree - 1.0) / (degree * degree - order * order))
    below = degree - 1.0
    back = jnp.sqrt(
        jnp.maximum(below * below - order * order, 0.0) / jnp.abs(4.0 * below * below - 1.0)
    )
    return (top, top * back)


def legendre_blocks(orders, cosine_lat, sine_lat):
    order_total = orders.shape[0]
    lat_total = cosine_lat.shape[0]
    block_total = 16
    block_length = DSLOT // block_total
    order_grid = orders[:, None, None]
    cosine_grid = cosine_lat[None, :, None]
    block_base = (jnp.arange(block_total) * block_length).astype(jnp.float32)[None, None, :]
    unit = jnp.ones((order_total, lat_total, block_total), jnp.float32)
    empty = jnp.zeros_like(unit)

    def compose(position, matrices):
        upper_left, upper_right, lower_left, lower_right = matrices
        top, mixed = step_factors(
            order_grid, order_grid + block_base + position.astype(jnp.float32)
        )
        diagonal_term = top * cosine_grid
        return (
            diagonal_term * upper_left - mixed * lower_left,
            diagonal_term * upper_right - mixed * lower_right,
            upper_left,
            upper_right,
        )

    upper_left, upper_right, lower_left, lower_right = lax.fori_loop(
        1, block_length + 1, compose, (unit, empty, empty, unit)
    )
    current = start_value(orders[:, None], sine_lat[None, :])
    previous = jnp.zeros_like(current)
    current_list = []
    previous_list = []
    for block in range(block_total):
        current_list.append(current)
        previous_list.append(previous)
        current, previous = (
            upper_left[:, :, block] * current + upper_right[:, :, block] * previous,
            lower_left[:, :, block] * current + lower_right[:, :, block] * previous,
        )
    current = jnp.stack(current_list, axis=-1)
    previous = jnp.stack(previous_list, axis=-1)
    outputs = []
    for position in range(1, block_length + 1):
        outputs.append(current)
        top, mixed = step_factors(order_grid, order_grid + block_base + float(position))
        current, previous = (top * cosine_grid * current - mixed * previous, current)
    values = jnp.stack(outputs, axis=-1)
    return values.reshape(order_total, lat_total, DSLOT)


def weighted_basis(orders, cosine_lat, sine_lat, weight):
    values = legendre_blocks(orders, cosine_lat, sine_lat)
    offsets = jnp.arange(DSLOT).astype(jnp.float32)
    keep = (orders[:, None] + offsets[None, :] <= TRUNC).astype(jnp.float32)
    factor = jnp.where(orders > 0, math.sqrt(2.0), 1.0)
    table = values * keep[:, None, :] * weight[None, :, None] * factor[:, None, None]
    return table.astype(jnp.bfloat16)


def local(fields):
    row_count, month_count, lon_count = fields.shape
    lat_devices = lax.axis_size("lat")
    slots_dev = MSLOT // lat_devices
    lat_index = lax.axis_index("lat")
    column = jnp.arange(2 * MSLOT)
    group = column // (2 * slots_dev)
    inner = column % (2 * slots_dev) // 2
    part_index = column % 2
    own_inner = jnp.arange(slots_dev)
    wave_order = group * slots_dev + inner
    own_order = lat_index * slots_dev + own_inner
    longitude = jnp.arange(lon_count)
    phase = (
        2.0
        * math.pi
        * (wave_order[:, None] * longitude[None, :] % lon_count).astype(jnp.float32)
        / lon_count
    )
    active = (wave_order <= TRUNC).astype(jnp.float32)[:, None]
    transform = (
        jnp.where(part_index[:, None] == 0, jnp.cos(phase), -jnp.sin(phase))
        * active
        / math.sqrt(lon_count)
    )
    transform = transform.astype(jnp.bfloat16)
    flat_fields = fields.reshape(row_count * month_count, lon_count)
    fourier = lax.dot_general(
        transform, flat_fields, (((1,), (1,)), ((), ())), preferred_element_type=jnp.float32
    )
    fourier = fourier.astype(jnp.bfloat16).reshape(2 * MSLOT, row_count, month_count)
    moved = lax.all_to_all(fourier, "lat", split_axis=0, concat_axis=1, tiled=True)
    lat_count = moved.shape[1]
    theta = math.pi * (jnp.arange(lat_count).astype(jnp.float32) + 0.5) / lat_count
    cosine_lat = jnp.cos(theta)
    sine_lat = jnp.sin(theta)
    weight = math.pi * sine_lat / lat_count
    basis = weighted_basis(own_order.astype(jnp.float32), cosine_lat, sine_lat, weight)
    moved_data = moved.reshape(slots_dev, 2, lat_count, month_count)
    coefficients = jnp.einsum(
        "srjt,sjd->tsrd", moved_data, basis, preferred_element_type=jnp.float32
    )
    coefficients = coefficients.astype(jnp.bfloat16).reshape(month_count, -1)
    tm_devices = lax.axis_size("tm")
    total_months = month_count * tm_devices
    columns = lax.all_to_all(coefficients, "tm", split_axis=1, concat_axis=0, tiled=True)
    partial_gram = lax.psum_scatter(
        lax.dot_general(
            columns, columns, (((1,), (1,)), ((), ())), preferred_element_type=jnp.float32
        ),
        "tm",
        scatter_dimension=0,
        tiled=True,
    )
    gram = lax.psum(partial_gram, "lat")
    own_block = lax.dynamic_slice_in_dim(gram, lax.axis_index("tm") * month_count, month_count, 1)
    trace_total = lax.psum(jnp.sum(jnp.diagonal(own_block)), "tm")
    return total_months * gram / (trace_total + 1e-06)


def solution(mesh):
    placed = (P("lat", "tm", None),)
    return jax.shard_map(
        local, mesh=mesh, in_specs=placed, out_specs=P("tm", None), check_vma=False
    )
```

profile of v0, /device:TPU:0, one launch (start us, length us, event | category | flops | bytes accessed | tf_op | source)
XLA Modules:
  0.0 353.8 jit_solution(13318265986543368269)
XLA Ops:
  6.6 1.5 copy-done
  8.1 16.4 %convolution_convert_fusion = bf16[768,1024]{1,0:T(8,128)(2,1)} fusion(bf16[1024,1024]{1,0:T(8,128)(2,1)S(1)} %bitcast.84, f32[768]{0:T(1024)S(1)} %get-tuple-element.432, s32[768]{0:T(1024)S(1)} %fusion.324, pred[768]{0:T(1024)(128)(4,1)S(1)} %get-tuple-element.431), kind=kOutput, calls=%fused_computation.41 | convolution fusion | flops 1626341376 | bytes 3676928 | tf_op jit(solution)/shard_map/dot_general | solution.py:118
  24.5 1.7 copy.127
  26.2 9.2 %copy.128 = bf16[768,32,32]{2,1,0:T(8,128)(2,1)} copy(bf16[768,32,32]{0,2,1:T(8,128)(2,1)S(1)} %bitcast.90) | data formatting | bytes 3145728 | tf_op jit(solution)/shard_map/reshape | solution.py:121
  35.4 9.3 %reshape.8823 = bf16[16,2,24576]{2,1,0:T(2,128)(2,1)} reshape(bf16[768,32,32]{2,1,0:T(8,128)(2,1)} %copy.128) | data formatting | bytes 3145728
  44.7 7.4 %all-to-all-start = ((bf16[16,2,24576]{2,1,0:T(2,128)(2,1)}), bf16[16,2,24576]{2,1,0:T(2,128)(2,1)}, u32[]{:S(2)}, u32[]{:S(2)}) async-start(bf16[16,2,24576]{2,1,0:T(2,128)(2,1)} %reshape.8823), calls=%async_computation | async-start | bytes 3145728 | tf_op jit(solution)/shard_map/all_to_all | solution.py:122
  53.3 71.6 %while.25 = (s32[]{:T(128)}, f32[24,512,16]{1,2,0:T(8,128)S(1)}, f32[24,512,16]{1,2,0:T(8,128)}, f32[24,512,16]{1,2,0:T(8,128)S(1)}, f32[24,512,16]{1,2,0:T(8,128)S(1)}, /*index=5*/s32[]{:T(128)}, s32[]{:T(128)}, s32[]{:T(128)}) while((s32[]{:T(128)}, f32[24,512,16]{1,2,0:T(8,128)S(1)}, ...), condition=%wide.region_1.2_spmd.clone.clone.clone, body=%wide.region_0.1_spmd.clone.clone.clone.sunk | while | flops 1778076 | bytes 6308475 | solution.py:57
  53.6 1.5 fusion.362
  55.5 2.7 fusion.362
  58.6 2.7 fusion.362
  61.6 2.7 fusion.362
  64.6 2.7 fusion.362
  67.6 2.7 fusion.362
  70.7 2.7 fusion.362
  73.7 2.7 fusion.362
  76.7 2.7 fusion.362
  79.8 2.7 fusion.362
  82.8 2.7 fusion.362
  85.8 2.7 fusion.362
  88.8 2.7 fusion.362
  91.9 2.7 fusion.362
  94.9 2.7 fusion.362
  97.9 2.7 fusion.362
  101.0 2.7 fusion.362
  104.0 2.7 fusion.362
  107.0 2.7 fusion.362
  110.0 2.7 fusion.362
  113.1 2.7 fusion.362
  116.1 2.7 fusion.362
  119.1 2.7 fusion.362
  122.1 2.7 fusion.362
  125.6 6.1 %add_bitcast_fusion = (f32[24,512,1,1]{1,2,3,0:T(1,128)S(1)}, f32[24,512,1]{1,2,0:T(1,128)S(1)}, f32[24,512,1]{1,2,0:T(1,128)S(1)}, f32[24,512,1]{1,2,0:T(1,128)...) fusion(f32[24,512,16]{1,2,0:T(8,128)S(1)} %get-tuple-element.24, ...), kind=kLoop, calls=%fused_computation.123 | loop fusion | flops 1155072 | bytes 4278464 | tf_op jit(solution)/shard_map/stack | solution.py:72
  132.9 1.3 stack.130
  150.8 2.0 stack.148
  152.9 3.0 stack.164
  157.1 1.2 constant_dynamic-update-slice_fusion.17
  158.3 2.1 constant_dynamic-update-slice_fusion.16
  160.3 2.0 constant_dynamic-update-slice_fusion.15
  163.4 1.2 constant_dynamic-update-slice_fusion.13
  164.6 2.1 constant_dynamic-update-slice_fusion.12
  166.7 1.3 constant_dynamic-update-slice_fusion.11
  169.1 1.2 constant_dynamic-update-slice_fusion.9
  170.3 1.3 constant_dynamic-update-slice_fusion.8
  171.6 1.3 constant_dynamic-update-slice_fusion.7
  174.0 1.2 constant_dynamic-update-slice_fusion.5
  175.2 1.3 constant_dynamic-update-slice_fusion.4
  176.6 1.4 constant_dynamic-update-slice_fusion.3
  179.0 1.2 constant_dynamic-update-slice_fusion.1
  180.2 1.2 constant_dynamic-update-slice_fusion
  183.0 1.2 fusion.36
  184.2 1.3 fusion.35
  185.4 1.4 subtract_dynamic-update-slice_fusion
  186.8 17.4 %copy.126 = f32[24,512,16,24]{1,3,2,0:T(8,128)S(1)} copy(f32[24,512,16,24]{1,2,3,0:T(8,128)} %subtract_dynamic-update-slice_fusion) | data formatting | bytes 37748736 | tf_op jit(solution)/shard_map/stack | solution.py:78
  204.4 6.3 %fusion.20 = bf16[24,512,384]{1,2,0:T(8,128)(2,1)} fusion(f32[24,512,16,24]{1,3,2,0:T(8,128)S(1)} %copy.126, f32[24]{0:T(128)S(1)} %copy-done.23, f32[512]{0:T(512)S(1)} %fusion.337, f32[24,384]{1,0:T(8,128)S(1)} %fusion.38), kind=kLoop, calls=%fused_computation.30 | loop fusion | flops 18874368 | bytes 28350560 | tf_op jit(solution)/shard_map/convert_element_type | solution.py:88
  210.6 7.9 %reshape.8824 = bf16[768,32,32]{2,1,0:T(8,128)(2,1)} reshape(bf16[16,2,24576]{2,1,0:T(2,128)(2,1)} %all-to-all-done) | data formatting | bytes 3145728
  218.5 9.5 %copy.129 = bf16[16,48,32,32]{2,0,3,1:T(8,128)(2,1)} copy(bf16[16,48,32,32]{3,2,1,0:T(8,128)(2,1)} %bitcast.85) | data formatting | bytes 3145728 | tf_op jit(solution)/shard_map/all_to_all | solution.py:122
  228.0 9.3 %reshape.8814 = bf16[24,2,512,32]{2,3,1,0:T(8,128)(2,1)} reshape(bf16[48,16,32,32]{2,1,3,0:T(8,128)(2,1)} %bitcast.86) | data formatting | bytes 3145728 | tf_op jit(solution)/shard_map/reshape | solution.py:129
  237.3 7.0 %fusion.352 = f32[24,384,64]{1,2,0:S(1)} fusion(bf16[24,512,384]{1,2,0:T(8,128)(2,1)} %fusion.20, bf16[24,512,64]{1,2,0:T(8,128)(2,1)} %bitcast.89), kind=kOutput, calls=%fused_computation.517 | convolution fusion | flops 603979776 | bytes 13369344
  245.5 1.6 all_to_all.28
  247.1 1.5 copy.132
  248.6 18.3 %all_to_all.34 = bf16[32,2,9216]{2,0,1:T(8,128)(2,1)S(1)} all-to-all(bf16[32,2,9216]{2,0,1:T(8,128)(2,1)S(1)} %copy.132), channel_id=1, replica_groups=mesh['lat'=16,'tm'=2] {'tm'}, dimensions={1} | all-to-all | bytes 2359296 | tf_op jit(solution)/shard_map/all_to_all | solution.py:136
  267.9 10.2 %reduce-scatter.2.cloned.1.call-done = f32[32,64]{1,0:T(8,128)} async-done(((f32[64,64]{1,0:T(8,128)}), f32[32,64]{1,0:T(8,128)}) %reduce-scatter.2.cloned.1.call-update) | async-done | bytes 8208 | tf_op jit(solution)/shard_map/reduce_scatter | solution.py:137
  278.1 60.6 %psum.14 = f32[32,64]{1,0:T(8,128)S(1)} all-reduce(f32[32,64]{1,0:T(8,128)} %reduce-scatter.2.cloned.1.call-done), channel_id=1, replica_groups=mesh['lat'=16,'tm'=2] {'lat'}, use_global_device_ids=true, to_apply=%region_3.4 | all-reduce | flops 2048 | bytes 16384 | tf_op jit(solution)/shard_map/psum | solution.py:145
  340.1 5.5 %psum.15 = f32[]{:T(128)} all-reduce(f32[]{:T(128)} %reduce_sum.9), channel_id=1, replica_groups=mesh['lat'=16,'tm'=2] {'tm'}, use_global_device_ids=true, to_apply=%region_5.6 | all-reduce | flops 1 | bytes 8 | tf_op jit(solution)/shard_map/psum | solution.py:147
  (298 shorter events, 39.0 us)
Async XLA Ops:
  6.5 1.6 copy-start
  44.7 165.9 %all-to-all-start = ((bf16[16,2,24576]{2,1,0:T(2,128)(2,1)}), bf16[16,2,24576]{2,1,0:T(2,128)(2,1)}, u32[]{:S(2)}, u32[]{:S(2)}) async-start(bf16[16,2,24576]{2,1,0:T(2,128)(2,1)} %reshape.8823), calls=%async_computation | async-start | bytes 3145728 | tf_op jit(solution)/shard_map/all_to_all | solution.py:122
  52.2 226.0 %reduce-scatter.2.cloned.1.call-start = ((), (), s32[]{:S(2)}) async-start(), calls=%async_computation.3 | async-start | bytes 49152 | tf_op jit(solution)/shard_map/reduce_scatter | solution.py:137
  52.4 82.7 %copy-start.21 = (f32[24]{0:T(128)}, f32[24]{0:T(128)S(1)}, u32[]{:S(2)}) copy-start(f32[24]{0:T(128)S(1)} %add_convert_fusion) | copy-start | bytes 292
  152.8 13.9 %copy-start.13 = (f32[24,16]{1,0:T(8,128)S(1)}, f32[24,16]{1,0:T(8,128)}, u32[]{:S(2)}) copy-start(f32[24,16]{1,0:T(8,128)} %copy.93) | copy-start | bytes 4612
  152.8 13.9 %copy-start.15 = (f32[24,16]{1,0:T(8,128)S(1)}, f32[24,16]{1,0:T(8,128)}, u32[]{:S(2)}) copy-start(f32[24,16]{1,0:T(8,128)} %copy.94) | copy-start | bytes 4612
  152.8 17.5 %copy-start.12 = (f32[24,16]{1,0:T(8,128)S(1)}, f32[24,16]{1,0:T(8,128)}, u32[]{:S(2)}) copy-start(f32[24,16]{1,0:T(8,128)} %copy.100) | copy-start | bytes 4612
  152.8 17.5 %copy-start.14 = (f32[24,16]{1,0:T(8,128)S(1)}, f32[24,16]{1,0:T(8,128)}, u32[]{:S(2)}) copy-start(f32[24,16]{1,0:T(8,128)} %copy.99) | copy-start | bytes 4612
  152.8 18.8 %copy-start.9 = (f32[24,16]{1,0:T(8,128)S(1)}, f32[24,16]{1,0:T(8,128)}, u32[]{:S(2)}) copy-start(f32[24,16]{1,0:T(8,128)} %copy.101) | copy-start | bytes 4612
  152.8 18.8 %copy-start.11 = (f32[24,16]{1,0:T(8,128)S(1)}, f32[24,16]{1,0:T(8,128)}, u32[]{:S(2)}) copy-start(f32[24,16]{1,0:T(8,128)} %copy.102) | copy-start | bytes 4612
  157.1 18.2 %copy-start.8 = (f32[24,16]{1,0:T(8,128)S(1)}, f32[24,16]{1,0:T(8,128)}, u32[]{:S(2)}) copy-start(f32[24,16]{1,0:T(8,128)} %copy.107) | copy-start | bytes 4612
  157.1 18.2 %copy-start.10 = (f32[24,16]{1,0:T(8,128)S(1)}, f32[24,16]{1,0:T(8,128)}, u32[]{:S(2)}) copy-start(f32[24,16]{1,0:T(8,128)} %copy.108) | copy-start | bytes 4612
  158.3 18.3 %copy-start.6 = (f32[24,16]{1,0:T(8,128)S(1)}, f32[24,16]{1,0:T(8,128)}, u32[]{:S(2)}) copy-start(f32[24,16]{1,0:T(8,128)} %copy.109) | copy-start | bytes 4612
  158.3 18.3 %copy-start.7 = (f32[24,16]{1,0:T(8,128)S(1)}, f32[24,16]{1,0:T(8,128)}, u32[]{:S(2)}) copy-start(f32[24,16]{1,0:T(8,128)} %copy.110) | copy-start | bytes 4612
  162.3 16.7 %copy-start.4 = (f32[24,16]{1,0:T(8,128)S(1)}, f32[24,16]{1,0:T(8,128)}, u32[]{:S(2)}) copy-start(f32[24,16]{1,0:T(8,128)} %copy.113) | copy-start | bytes 4612
  162.3 16.7 %copy-start.5 = (f32[24,16]{1,0:T(8,128)S(1)}, f32[24,16]{1,0:T(8,128)}, u32[]{:S(2)}) copy-start(f32[24,16]{1,0:T(8,128)} %copy.114) | copy-start | bytes 4612
  164.6 15.6 %copy-start.2 = (f32[24,16]{1,0:T(8,128)S(1)}, f32[24,16]{1,0:T(8,128)}, u32[]{:S(2)}) copy-start(f32[24,16]{1,0:T(8,128)} %copy.115) | copy-start | bytes 4612
  164.6 15.7 %copy-start.3 = (f32[24,16]{1,0:T(8,128)S(1)}, f32[24,16]{1,0:T(8,128)}, u32[]{:S(2)}) copy-start(f32[24,16]{1,0:T(8,128)} %copy.116) | copy-start | bytes 4612
  168.0 14.5 %copy-start.20 = (f32[24,16]{0,1:T(8,128)S(1)}, f32[24,16]{0,1:T(8,128)}, u32[]{:S(2)}) copy-start(f32[24,16]{0,1:T(8,128)} %get-tuple-element.404) | copy-start | bytes 4612
  168.0 14.6 %copy-start.19 = (f32[24,16]{0,1:T(8,128)S(1)}, f32[24,16]{0,1:T(8,128)}, u32[]{:S(2)}) copy-start(f32[24,16]{0,1:T(8,128)} %get-tuple-element.408) | copy-start | bytes 4612
  168.0 14.7 %copy-start.18 = (f32[24,16]{0,1:T(8,128)S(1)}, f32[24,16]{0,1:T(8,128)}, u32[]{:S(2)}) copy-start(f32[24,16]{0,1:T(8,128)} %get-tuple-element.405) | copy-start | bytes 4612
  168.0 14.7 %copy-start.17 = (f32[24,16]{0,1:T(8,128)S(1)}, f32[24,16]{0,1:T(8,128)}, u32[]{:S(2)}) copy-start(f32[24,16]{0,1:T(8,128)} %get-tuple-element.407) | copy-start | bytes 4612
  168.0 14.8 %copy-start.16 = (f32[24,16]{0,1:T(8,128)S(1)}, f32[24,16]{0,1:T(8,128)}, u32[]{:S(2)}) copy-start(f32[24,16]{0,1:T(8,128)} %get-tuple-element.383) | copy-start | bytes 4612
  186.8 17.5 %copy-start.22 = (f32[24]{0:T(128)S(1)}, f32[24]{0:T(128)}, u32[]{:S(2)}) copy-start(f32[24]{0:T(128)} %copy-done.21) | copy-start | bytes 292
  186.8 17.5 %copy-start.23 = (f32[24]{0:T(128)S(1)}, f32[24]{0:T(128)}, u32[]{:S(2)}) copy-start(f32[24]{0:T(128)} %get-tuple-element.429) | copy-start | bytes 292
  218.5 128.4 %copy-start.1 = (bf16[32,32,1024]{2,1,0:T(8,128)(2,1)S(1)}, bf16[32,32,1024]{2,1,0:T(8,128)(2,1)}, u32[]{:S(2)}) copy-start(bf16[32,32,1024]{2,1,0:T(8,128)(2,1)} %param.3) | copy-start | bytes 6291460
Sparse Core Ops, SparseCore 0:
  268.0 10.0 reduce-scatter.1
where the time goes:
time: 356 us; the launch traced here: 354 us
  other arithmetic  115 us (32%)
  local copies, waits for them, and re-layouts  96.8 us (27%)
  blocking collectives  84.4 us (24%)
  matrix products  24.4 us (7%)
  between operations  14.4 us (4%)
  waiting for transfers between devices  10.2 us (3%)
  starting transfers between devices  7.65 us (2%)
    sub x24, other arithmetic, compose(): diagonal_term * upper_right - mixed * lower_right  63.1 us
    psum x1, blocking collectives, local(): gram = lax.psum(partial_gram, 'lat')  60.6 us
    unnamed x24, other arithmetic  29 us
    unnamed x51, local copies, waits for them, and re-layouts  19.8 us
    all_to_all x1, blocking collectives, local(): lax.all_to_all(coefficients, 'tm', split_axis=1, concat_axis=0, tiled=True)  18.3 us
    another operation x1, local copies, waits for them, and re-layouts, legendre_blocks(): values = jnp.stack(outputs, axis=-1)  17.4 us
    dot_general x1, matrix products, local(): lax.dot_general(transform, flat_fields, (((1,), (1,)), ((), ())), preferr...  16.4 us
    reduce_scatter x1, waiting for transfers between devices, local(): lax.psum_scatter(lax.dot_general(columns, columns, (((1,), (1,)), ((), ()...  10.2 us
  transfers between devices with their start and end apart: 2, of which 1 were waited for; matrix products, arithmetic and copies ran while one was open for 45% of the time, Pallas kernels for 0%

commit v1 on v0

v1 whole, which is shorter than its diff:
```python
import functools
import math

import jax
import jax.numpy as jnp
import numpy as np
from jax import lax
from jax.experimental import pallas as pl
from jax.experimental.pallas import tpu as pltpu
from jax.sharding import PartitionSpec as P

TRUNC = 341
GROUP = 8
LANES = 128
HALF = 64
PIECE = 8
MESH = pl.DeviceIdType.MESH


def twiddle_table(device_total, slots, lon_count):
    groups = device_total // GROUP
    device = np.arange(device_total).reshape(groups, 1, GROUP, 1)
    slot = np.arange(slots).reshape(1, 1, 1, slots)
    wave = np.broadcast_to(slot * device_total + device, (groups, 1, GROUP, slots))
    longitude = np.arange(lon_count)
    phase = 2.0 * math.pi * ((wave[..., None] * longitude) % lon_count) / lon_count
    table = np.concatenate([np.cos(phase), -np.sin(phase)], axis=1)
    table = table * (wave[..., None] <= TRUNC) / math.sqrt(lon_count)
    table = table.reshape(groups, 2 * GROUP * slots, lon_count)
    return table.astype(np.float32).astype(jnp.bfloat16)


def start_table(device_total, slots, slot_rows):
    table = np.zeros((device_total, slot_rows), np.float64)
    for device in range(device_total):
        for slot in range(slot_rows):
            order = min(slot, slots - 1) * device_total + device
            table[device, slot] = 0.5 * (
                math.log(0.5)
                + math.lgamma(order + 1.5)
                - math.lgamma(1.5)
                - math.lgamma(order + 1.0)
            )
    table = np.broadcast_to(table[:, :, None], (device_total, slot_rows, LANES))
    return table.astype(np.float32)


def lat_table(lat_total, share):
    lat = np.arange(lat_total).reshape(lat_total // share, share).T.reshape(-1)
    theta = math.pi * (lat + 0.5) / lat_total
    table = np.stack([np.cos(theta), np.log(np.sin(theta)), math.pi * np.sin(theta) / lat_total])
    return table.reshape(3, lat_total // LANES, LANES).astype(np.float32)


def kernel(
    dims,
    x_ref,
    table_ref,
    start_ref,
    lat_ref,
    out_ref,
    spread,
    outbox,
    inbox,
    legendre,
    gram_ref,
    local_gram,
    parts,
    own_sum,
    full,
    send_sem,
    recv_sem,
    part_send,
    part_recv,
    sum_send,
    sum_recv,
):
    lat_devices, tm_devices, rows, months, lon_count, slots, slot_rows, depth = dims
    device_total = lat_devices * tm_devices
    groups = device_total // GROUP
    share = HALF // months
    high = rows // share
    lat_total = lat_devices * rows
    lat_groups = lat_total // LANES
    month_total = months * tm_devices
    pieces = month_total // PIECE
    stride = device_total // pieces
    lat_me = lax.axis_index("lat")
    tm_me = lax.axis_index("tm")
    me = lat_me * tm_devices + tm_me

    def coords(device):
        return (device // tm_devices, lax.rem(device, tm_devices))

    barrier = pltpu.get_barrier_semaphore()

    @pl.loop(1, device_total)
    def _(step):
        pl.semaphore_signal(
            barrier,
            inc=1,
            device_id=coords(lax.rem(me + step, device_total)),
            device_id_type=MESH,
        )

    group_rows = GROUP * slots
    lane = lax.broadcasted_iota(jnp.int32, (group_rows, LANES), 1)
    lower = lane < HALF

    @pl.loop(0, groups)
    def _(group):
        values = lax.dot_general(
            table_ref[group],
            x_ref[...],
            (((1,), (1,)), ((), ())),
            preferred_element_type=jnp.float32,
        )
        for block in range(rows * months // LANES):
            cosine = values[:group_rows, block * LANES : (block + 1) * LANES]
            sine = values[group_rows:, block * LANES : (block + 1) * LANES]
            even = jnp.where(lower, cosine, pltpu.roll(sine, HALF, 1))
            odd = jnp.where(lower, pltpu.roll(cosine, HALF, 1), sine)
            spread[pl.ds(2 * block, group_rows, stride=high), :] = even
            spread[pl.ds(2 * block + 1, group_rows, stride=high), :] = odd
        packed = spread[...].astype(jnp.bfloat16)
        outbox[pl.ds(group * GROUP, GROUP)] = packed.reshape(GROUP, slots, high, LANES)

    pl.semaphore_wait(barrier, device_total - 1)

    def exchange(target, source):
        return pltpu.make_async_remote_copy(
            src_ref=outbox.at[target],
            dst_ref=inbox.at[source],
            send_sem=send_sem.at[target],
            recv_sem=recv_sem.at[source],
            device_id=coords(target),
            device_id_type=MESH,
        )

    @pl.loop(1, device_total)
    def _(step):
        exchange(lax.rem(me + step, device_total), me).start()

    inbox[me] = outbox[me]

    halves = slot_rows // 8
    sub = lax.broadcasted_iota(jnp.int32, (8, LANES), 0)
    slot_of = [sub + 8 * half for half in range(halves)]
    order_int = [slot * device_total + me for slot in slot_of]
    order = [value.astype(jnp.float32) for value in order_int]
    cosine_lat = [jnp.broadcast_to(lat_ref[0, pl.ds(g, 1), :], (8, LANES)) for g in range(lat_groups)]
    current = []
    scale = []
    for half in range(halves):
        factor = jnp.where(order_int[half] > 0, math.sqrt(2.0), 1.0)
        for g in range(lat_groups):
            log_start = (
                start_ref[me, pl.ds(8 * half, 8), :]
                + order[half] * jnp.broadcast_to(lat_ref[1, pl.ds(g, 1), :], (8, LANES))
            )
            taper = jnp.clip((log_start + 70.0) / 10.0, 0.0, 1.0)
            current.append(jnp.exp(jnp.maximum(log_start, -80.0)) * taper)
            scale.append(factor * jnp.broadcast_to(lat_ref[2, pl.ds(g, 1), :], (8, LANES)))

    def store(offset, values):
        for half in range(halves):
            keep = (order_int[half] + offset <= TRUNC) & (slot_of[half] < slots)
            for g in range(lat_groups):
                index = half * lat_groups + g
                value = jnp.where(keep, values[index] * scale[index], 0.0)
                legendre[g, pl.ds(8 * half * depth + offset, 8, stride=depth), :] = value

    store(0, current)

    def advance(offset, carry):
        now, before, backs = carry
        real = lax.convert_element_type(offset, jnp.float32)
        following = []
        next_backs = []
        for half in range(halves):
            degree = order[half] + real
            ratio = (4.0 * degree * degree - 1.0) / (real * (order[half] + degree))
            top = jnp.sqrt(ratio)
            next_backs.append(1.0 / top)
            for g in range(lat_groups):
                index = half * lat_groups + g
                following.append(
                    top * (cosine_lat[g] * now[index] - backs[half] * before[index])
                )
        store(offset, following)
        return following, now, next_backs

    zero = jnp.zeros((8, LANES), jnp.float32)
    lax.fori_loop(
        1,
        depth,
        advance,
        (current, [zero] * len(current), [zero] * halves),
        unroll=7,
    )

    @pl.loop(1, device_total)
    def _(step):
        source = lax.rem(me + step, device_total)
        exchange(source, source).wait_recv()

    per_share = lat_groups // share
    width = tm_devices * LANES
    share_of = lax.broadcasted_iota(jnp.int32, (depth, width), 1) % HALF // months
    gram_ref[...] = jnp.zeros_like(gram_ref)

    @pl.loop(0, slots)
    def _(slot):
        received = jnp.concatenate(
            [
                jnp.concatenate(
                    [
                        inbox[lat_device * tm_devices + tm, slot]
                        for lat_device in range(lat_devices)
                    ],
                    axis=0,
                )
                for tm in range(tm_devices)
            ],
            axis=1,
        )
        first = pl.multiple_of(slot * depth, 8)
        merged = None
        for part in range(share):
            basis = jnp.concatenate(
                [
                    legendre[part * per_share + g, pl.ds(first, depth), :].astype(jnp.bfloat16)
                    for g in range(per_share)
                ],
                axis=1,
            )
            product = jnp.dot(basis, received, preferred_element_type=jnp.float32)
            merged = product if part == 0 else jnp.where(share_of == part, product, merged)
        total = merged
        for part in range(1, share):
            total = total + pltpu.roll(merged, width - part * months, 1)
        coefficients = jnp.where(share_of == 0, total, 0.0).astype(jnp.bfloat16)
        gram_ref[...] += lax.dot_general(
            coefficients,
            coefficients,
            (((0,), (0,)), ((), ())),
            preferred_element_type=jnp.float32,
        )

    gram = None
    for part in range(2):
        across = jnp.concatenate(
            [
                gram_ref[pl.ds(tm * LANES + part * HALF, months), :]
                for tm in range(tm_devices)
            ],
            axis=0,
        )
        block = jnp.concatenate(
            [
                across[:, tm * LANES + part * HALF : tm * LANES + part * HALF + months]
                for tm in range(tm_devices)
            ],
            axis=1,
        )
        gram = block if gram is None else gram + block
    local_gram[...] = gram.reshape(pieces, PIECE, month_total)

    def owner(piece):
        return piece * stride + stride // 2

    def send_part(piece, source):
        return pltpu.make_async_remote_copy(
            src_ref=local_gram.at[piece],
            dst_ref=parts.at[source],
            send_sem=part_send.at[piece],
            recv_sem=part_recv.at[source],
            device_id=coords(owner(piece)),
            device_id_type=MESH,
        )

    def send_sum(piece, target):
        return pltpu.make_async_remote_copy(
            src_ref=own_sum,
            dst_ref=full.at[piece],
            send_sem=sum_send.at[target],
            recv_sem=sum_recv.at[piece],
            device_id=coords(target),
            device_id_type=MESH,
        )

    @pl.loop(0, pieces)
    def _(piece):
        @pl.when(owner(piece) != me)
        def _():
            send_part(piece, me).start()

    my_piece = me // stride

    @pl.when(lax.rem(me, stride) == stride // 2)
    def _():
        parts[me] = local_gram[my_piece]

        @pl.loop(1, device_total)
        def _(step):
            source = lax.rem(me + step, device_total)
            send_part(my_piece, source).wait_recv()

        total = lax.fori_loop(
            0,
            device_total,
            lambda source, value: value + parts[source],
            jnp.zeros((PIECE, month_total), jnp.float32),
        )
        own_sum[...] = total
        full[my_piece] = total

        @pl.loop(1, device_total)
        def _(step):
            send_sum(my_piece, lax.rem(me + step, device_total)).start()

    @pl.loop(0, pieces)
    def _(piece):
        @pl.when(owner(piece) != me)
        def _():
            send_sum(piece, me).wait_recv()

    gram = full[...].reshape(month_total, month_total)
    on_diagonal = lax.broadcasted_iota(jnp.int32, gram.shape, 0) == lax.broadcasted_iota(
        jnp.int32, gram.shape, 1
    )
    trace = jnp.sum(jnp.where(on_diagonal, gram, 0.0))
    mine = full[pl.ds(tm_me * (months // PIECE), months // PIECE)].reshape(months, month_total)
    out_ref[...] = month_total * mine / (trace + 1e-06)

    @pl.loop(1, device_total)
    def _(step):
        exchange(lax.rem(me + step, device_total), me).wait_send()

    @pl.loop(0, pieces)
    def _(piece):
        @pl.when(owner(piece) != me)
        def _():
            send_part(piece, me).wait_send()

    @pl.when(lax.rem(me, stride) == stride // 2)
    def _():
        @pl.loop(1, device_total)
        def _(step):
            send_sum(my_piece, lax.rem(me + step, device_total)).wait_send()


def solution(mesh):
    lat_devices = mesh.shape["lat"]
    tm_devices = mesh.shape["tm"]
    device_total = lat_devices * tm_devices
    slots = -(-(TRUNC + 1) // device_total)
    slot_rows = -(-slots // 8) * 8
    depth = -(-(TRUNC + 1) // 8) * 8

    def local(fields):
        rows, months, lon_count = fields.shape
        month_total = months * tm_devices
        lat_total = rows * lat_devices
        share = HALF // months
        high = rows // share
        pieces = month_total // PIECE
        width = tm_devices * LANES
        dims = (lat_devices, tm_devices, rows, months, lon_count, slots, slot_rows, depth)
        table = jnp.asarray(twiddle_table(device_total, slots, lon_count))
        starts = jnp.asarray(start_table(device_total, slots, slot_rows))
        lats = jnp.asarray(lat_table(lat_total, share))
        vmem = pl.BlockSpec(memory_space=pltpu.VMEM)
        dma = pltpu.SemaphoreType.DMA
        return pl.pallas_call(
            functools.partial(kernel, dims),
            out_shape=jax.ShapeDtypeStruct((months, month_total), jnp.float32),
            in_specs=[vmem] * 4,
            out_specs=vmem,
            scratch_shapes=[
                pltpu.VMEM((GROUP * slots * high, LANES), jnp.float32),
                pltpu.VMEM((device_total, slots, high, LANES), jnp.bfloat16),
                pltpu.VMEM((device_total, slots, high, LANES), jnp.bfloat16),
                pltpu.VMEM((lat_total // LANES, slot_rows * depth, LANES), jnp.float32),
                pltpu.VMEM((width, width), jnp.float32),
                pltpu.VMEM((pieces, PIECE, month_total), jnp.float32),
                pltpu.VMEM((device_total, PIECE, month_total), jnp.float32),
                pltpu.VMEM((PIECE, month_total), jnp.float32),
                pltpu.VMEM((pieces, PIECE, month_total), jnp.float32),
                dma((device_total,)),
                dma((device_total,)),
                dma((pieces,)),
                dma((device_total,)),
                dma((device_total,)),
                dma((pieces,)),
            ],
            compiler_params=pltpu.CompilerParams(
                collective_id=0, has_side_effects=True, vmem_limit_bytes=60 * 1024 * 1024
            ),
        )(fields.reshape(rows * months, lon_count), table, starts, lats)

    return jax.shard_map(
        local, mesh=mesh, in_specs=(P("lat", "tm", None),), out_specs=P("tm", None), check_vma=False
    )
```

time: 356 us -> 60.5 us (0.17)
  other arithmetic: 115 us -> 0 us
  local copies, waits for them, and re-layouts: 96.8 us -> 1.32 us
  blocking collectives: 84.4 us -> 0 us
  Pallas kernels: 0 us -> 58.9 us
  matrix products: 24.4 us -> 0 us
  between operations: 14.4 us -> 0.01 us
  waiting for transfers between devices: 10.2 us -> 0 us
  starting transfers between devices: 7.65 us -> 0 us
    psum x2 -> x0, blocking collectives: 66.2 us -> none  [the longest x1 60.6 us: local(): gram = lax.psum(partial_gram, 'lat')]
    sub x48 -> x0, other arithmetic: 63.3 us -> none  [the longest x24 63.1 us: compose(): diagonal_term * upper_right - mixed * lower_right]
    pallas_call x0 -> x1, Pallas kernels: none -> 58.9 us  [local(): pl.pallas_call(functools.partial(kernel, dims), out_shape=jax.ShapeDtypeS...]
    unnamed x24 -> x0, other arithmetic: 29 us -> none
    another operation x5 -> x0, local copies, waits for them, and re-layouts: 23.7 us -> none  [the longest x1 17.4 us: legendre_blocks(): values = jnp.stack(outputs, axis=-1)]
    unnamed x51 -> x1, local copies, waits for them, and re-layouts: 19.8 us -> 1.32 us
    reshape x2 -> x0, local copies, waits for them, and re-layouts: 18.5 us -> none  [the longest x1 9.28 us: local(): moved_data = moved.reshape(slots_dev, 2, lat_count, month_count)]
    all_to_all x1 -> x0, blocking collectives: 18.3 us -> none  [local(): lax.all_to_all(coefficients, 'tm', split_axis=1, concat_axis=0, tiled=True)]
  transfers between devices with their start and end apart: 2 -> 0, of which waited for: 1 -> 0; matrix products, arithmetic and copies ran while one was open for 45% -> 0% of each run, Pallas kernels for 0% -> 0%
where the time goes in v1:
time: 60.5 us; the launch traced here: 60.2 us
  Pallas kernels  58.9 us (97%)
  local copies, waits for them, and re-layouts  1.32 us (2%)
    pallas_call x1, Pallas kernels, local(): pl.pallas_call(functools.partial(kernel, dims), out_shape=jax.ShapeDtypeS...  58.9 us
    unnamed x1, local copies, waits for them, and re-layouts  1.32 us

profile of v1, /device:TPU:0, one launch (start us, length us, event | category | flops | bytes accessed | tf_op | source)
XLA Modules:
  0.0 60.2 jit_solution(13529912083454089190)
XLA Ops:
  0.0 58.9 %shard_map.46 = f32[32,64]{1,0:T(8,128)} custom-call(bf16[1024,1024]{1,0:T(8,128)(2,1)} %bitcast.1, bf16[4,176,1024]{2,1,0:T(8,128)(2,1)} %constant.6.clone.table_ref, f32[32,16,128]{2,1,0:T(8,128)} %constant.7.clone.start_ref, f32[3,4,128]{2,1,0:T(4,128)} %constant.8.clone.lat_ref), custom_call_target="tpu_custom_call" | custom-call | tf_op jit(solution)/shard_map/pallas_call | solution.py:375
  58.9 1.3 %copy.6 = f32[32,64]{1,0:T(8,128)} copy(f32[32,64]{1,0:T(8,128)} %shard_map.46) | data formatting | bytes 16384

commit v2 on v1

--- a/solution.py
+++ b/solution.py
@@ -14,6 +14,7 @@
 LANES = 128
 HALF = 64
 PIECE = 8
+PHASES = 4
 MESH = pl.DeviceIdType.MESH
 
 
@@ -45,6 +46,28 @@
     return table.astype(np.float32)
 
 
+def needed_slots(lat_devices, device_total, slots, rows):
+    counts = []
+    order = np.arange(slots * device_total)
+    rise = np.array(
+        [math.lgamma(m + 1.5) - math.lgamma(1.5) - math.lgamma(m + 1.0) for m in order]
+    )
+    for device in range(lat_devices):
+        lat = device * rows + np.arange(rows)
+        sine = np.sin(math.pi * (lat + 0.5) / (lat_devices * rows))
+        start = 0.5 * (math.log(0.5) + rise[:, None]) + order[:, None] * np.log(sine)[None, :]
+        used = (start > -70.5) & (order <= TRUNC)[:, None]
+        used = used.reshape(slots, -1).any(axis=1)
+        counts.append(int(np.max(np.nonzero(used)[0])) + 1 if used.any() else 0)
+    runs = []
+    for device, count in enumerate(counts):
+        if runs and runs[-1][2] == count:
+            runs[-1][1] = device + 1
+        else:
+            runs.append([device, device + 1, count])
+    return tuple(tuple(run) for run in runs)
+
+
 def lat_table(lat_total, share):
     lat = np.arange(lat_total).reshape(lat_total // share, share).T.reshape(-1)
     theta = math.pi * (lat + 0.5) / lat_total
@@ -54,11 +77,14 @@
 
 def kernel(
     dims,
-    x_ref,
-    table_ref,
+    runs,
+    x_hbm,
+    table_hbm,
     start_ref,
     lat_ref,
     out_ref,
+    x_ref,
+    table_ref,
     spread,
     outbox,
     inbox,
@@ -68,6 +94,8 @@
     parts,
     own_sum,
     full,
+    x_sem,
+    table_sem,
     send_sem,
     recv_sem,
     part_send,
@@ -84,13 +112,26 @@
     lat_groups = lat_total // LANES
     month_total = months * tm_devices
     pieces = month_total // PIECE
-    stride = device_total // pieces
+    stride = device_total // 2 // pieces
+    first_owner = device_total // 4
     lat_me = lax.axis_index("lat")
     tm_me = lax.axis_index("tm")
     me = lat_me * tm_devices + tm_me
 
     def coords(device):
         return (device // tm_devices, lax.rem(device, tm_devices))
+
+    x_copy = pltpu.make_async_copy(x_hbm, x_ref, x_sem)
+    x_copy.start()
+
+    def table_copy(group):
+        return pltpu.make_async_copy(
+            table_hbm.at[group], table_ref.at[group], table_sem.at[group]
+        )
+
+    @pl.loop(0, groups)
+    def _(group):
+        table_copy(group).start()
 
     barrier = pltpu.get_barrier_semaphore()
 
@@ -107,8 +148,18 @@
     lane = lax.broadcasted_iota(jnp.int32, (group_rows, LANES), 1)
     lower = lane < HALF
 
+    for first, last, count in runs:
+        if count < slots:
+
+            @pl.loop(first * tm_devices, last * tm_devices)
+            def _(source):
+                inbox[source, count:] = jnp.zeros((slots - count, high, LANES), jnp.bfloat16)
+
+    x_copy.wait()
+
     @pl.loop(0, groups)
     def _(group):
+        table_copy(group).wait()
         values = lax.dot_general(
             table_ref[group],
             x_ref[...],
@@ -127,19 +178,33 @@
 
     pl.semaphore_wait(barrier, device_total - 1)
 
-    def exchange(target, source):
+    phase_length = -(-slots // PHASES)
+    phases = [(low, min(low + phase_length, slots)) for low in range(0, slots, phase_length)]
+
+    def exchange(phase, count, target, source):
+        low, top = phases[phase]
+        span = pl.ds(low, min(count, top) - low)
         return pltpu.make_async_remote_copy(
-            src_ref=outbox.at[target],
-            dst_ref=inbox.at[source],
-            send_sem=send_sem.at[target],
-            recv_sem=recv_sem.at[source],
+            src_ref=outbox.at[target, span],
+            dst_ref=inbox.at[source, span],
+            send_sem=send_sem.at[phase, target],
+            recv_sem=recv_sem.at[phase, source],
             device_id=coords(target),
             device_id_type=MESH,
         )
 
-    @pl.loop(1, device_total)
-    def _(step):
-        exchange(lax.rem(me + step, device_total), me).start()
+    def each_send(act):
+        for phase in range(len(phases)):
+            for first, last, count in runs:
+                if count > phases[phase][0]:
+
+                    @pl.when((lat_me >= first) & (lat_me < last))
+                    def _():
+                        @pl.loop(1, device_total)
+                        def _(step):
+                            act(exchange(phase, count, lax.rem(me + step, device_total), me))
+
+    each_send(lambda copy: copy.start())
 
     inbox[me] = outbox[me]
 
@@ -199,18 +264,12 @@
         unroll=7,
     )
 
-    @pl.loop(1, device_total)
-    def _(step):
-        source = lax.rem(me + step, device_total)
-        exchange(source, source).wait_recv()
-
     per_share = lat_groups // share
     width = tm_devices * LANES
     share_of = lax.broadcasted_iota(jnp.int32, (depth, width), 1) % HALF // months
     gram_ref[...] = jnp.zeros_like(gram_ref)
 
-    @pl.loop(0, slots)
-    def _(slot):
+    def add_slot(slot):
         received = jnp.concatenate(
             [
                 jnp.concatenate(
@@ -247,6 +306,18 @@
             preferred_element_type=jnp.float32,
         )
 
+    for phase, (low, top) in enumerate(phases):
+        for first, last, count in runs:
+            if count > low:
+
+                @pl.loop(first * tm_devices, last * tm_devices)
+                def _(source):
+                    @pl.when(source != me)
+                    def _():
+                        exchange(phase, count, source, source).wait_recv()
+
+        pl.loop(low, top)(add_slot)
+
     gram = None
     for part in range(2):
         across = jnp.concatenate(
@@ -267,7 +338,7 @@
     local_gram[...] = gram.reshape(pieces, PIECE, month_total)
 
     def owner(piece):
-        return piece * stride + stride // 2
+        return first_owner + piece * stride
 
     def send_part(piece, source):
         return pltpu.make_async_remote_copy(
@@ -295,9 +366,14 @@
         def _():
             send_part(piece, me).start()
 
-    my_piece = me // stride
-
-    @pl.when(lax.rem(me, stride) == stride // 2)
+    is_owner = (
+        (me >= first_owner)
+        & (me < first_owner + pieces * stride)
+        & (lax.rem(me - first_owner + device_total, stride) == 0)
+    )
+    my_piece = lax.rem(me - first_owner + device_total, device_total) // stride
+
+    @pl.when(is_owner)
     def _():
         parts[me] = local_gram[my_piece]
 
@@ -333,9 +409,7 @@
     mine = full[pl.ds(tm_me * (months // PIECE), months // PIECE)].reshape(months, month_total)
     out_ref[...] = month_total * mine / (trace + 1e-06)
 
-    @pl.loop(1, device_total)
-    def _(step):
-        exchange(lax.rem(me + step, device_total), me).wait_send()
+    each_send(lambda copy: copy.wait_send())
 
     @pl.loop(0, pieces)
     def _(piece):
@@ -343,7 +417,7 @@
         def _():
             send_part(piece, me).wait_send()
 
-    @pl.when(lax.rem(me, stride) == stride // 2)
+    @pl.when(is_owner)
     def _():
         @pl.loop(1, device_total)
         def _(step):
@@ -370,14 +444,19 @@
         table = jnp.asarray(twiddle_table(device_total, slots, lon_count))
         starts = jnp.asarray(start_table(device_total, slots, slot_rows))
         lats = jnp.asarray(lat_table(lat_total, share))
+        runs = needed_slots(lat_devices, device_total, slots, rows)
+        phases = -(-slots // -(-slots // PHASES))
+        hbm = pl.BlockSpec(memory_space=pl.ANY)
         vmem = pl.BlockSpec(memory_space=pltpu.VMEM)
         dma = pltpu.SemaphoreType.DMA
         return pl.pallas_call(
-            functools.partial(kernel, dims),
+            functools.partial(kernel, dims, runs),
             out_shape=jax.ShapeDtypeStruct((months, month_total), jnp.float32),
-            in_specs=[vmem] * 4,
+            in_specs=[hbm, hbm, vmem, vmem],
             out_specs=vmem,
             scratch_shapes=[
+                pltpu.VMEM((rows * months, lon_count), jnp.bfloat16),
+                pltpu.VMEM(table.shape, jnp.bfloat16),
                 pltpu.VMEM((GROUP * slots * high, LANES), jnp.float32),
                 pltpu.VMEM((device_total, slots, high, LANES), jnp.bfloat16),
                 pltpu.VMEM((device_total, slots, high, LANES), jnp.bfloat16),
@@ -387,8 +466,10 @@
                 pltpu.VMEM((device_total, PIECE, month_total), jnp.float32),
                 pltpu.VMEM((PIECE, month_total), jnp.float32),
                 pltpu.VMEM((pieces, PIECE, month_total), jnp.float32),
-                dma((device_total,)),
-                dma((device_total,)),
+                dma,
+                dma((table.shape[0],)),
+                dma((phases, device_total)),
+                dma((phases, device_total)),
                 dma((pieces,)),
                 dma((device_total,)),
                 dma((device_total,)),

time: 60.5 us -> 50 us (0.83)
  Pallas kernels: 58.9 us -> 48.4 us
    pallas_call x1, Pallas kernels: 58.9 us -> 48.4 us  [local(): pl.pallas_call(functools.partial(kernel, dims, runs), out_shape=jax.Shape...]
where the time goes in v2:
time: 50 us; the launch traced here: 49.8 us
  Pallas kernels  48.4 us (97%)
  local copies, waits for them, and re-layouts  1.32 us (3%)
    pallas_call x1, Pallas kernels, local(): pl.pallas_call(functools.partial(kernel, dims, runs), out_shape=jax.Shape...  48.4 us
    unnamed x1, local copies, waits for them, and re-layouts  1.32 us

profile of v2, /device:TPU:0, one launch (start us, length us, event | category | flops | bytes accessed | tf_op | source)
XLA Modules:
  0.0 49.8 jit_solution(3245147923398391396)
XLA Ops:
  0.0 48.4 %shard_map.46 = f32[32,64]{1,0:T(8,128)} custom-call(bf16[1024,1024]{1,0:T(8,128)(2,1)} %bitcast.1, bf16[4,176,1024]{2,1,0:T(8,128)(2,1)} %constant.6.clone.table_hbm, f32[32,16,128]{2,1,0:T(8,128)} %constant.7.clone.start_ref, f32[3,4,128]{2,1,0:T(4,128)} %constant.8.clone.lat_ref), custom_call_target="tpu_custom_call" | custom-call | tf_op jit(solution)/shard_map/pallas_call | solution.py:452
  48.5 1.3 %copy.6 = f32[32,64]{1,0:T(8,128)} copy(f32[32,64]{1,0:T(8,128)} %shard_map.46) | data formatting | bytes 16384

commit v3 on v2

--- a/solution.py
+++ b/solution.py
@@ -10,7 +10,6 @@
 from jax.sharding import PartitionSpec as P
 
 TRUNC = 341
-GROUP = 8
 LANES = 128
 HALF = 64
 PIECE = 8
@@ -18,17 +17,21 @@
 MESH = pl.DeviceIdType.MESH
 
 
+def phase_bounds(slots):
+    length = -(-slots // PHASES)
+    return [(low, min(low + length, slots)) for low in range(0, slots, length)]
+
+
 def twiddle_table(device_total, slots, lon_count):
-    groups = device_total // GROUP
-    device = np.arange(device_total).reshape(groups, 1, GROUP, 1)
-    slot = np.arange(slots).reshape(1, 1, 1, slots)
-    wave = np.broadcast_to(slot * device_total + device, (groups, 1, GROUP, slots))
     longitude = np.arange(lon_count)
-    phase = 2.0 * math.pi * ((wave[..., None] * longitude) % lon_count) / lon_count
-    table = np.concatenate([np.cos(phase), -np.sin(phase)], axis=1)
-    table = table * (wave[..., None] <= TRUNC) / math.sqrt(lon_count)
-    table = table.reshape(groups, 2 * GROUP * slots, lon_count)
-    return table.astype(np.float32).astype(jnp.bfloat16)
+    parts = []
+    for low, top in phase_bounds(slots):
+        device = np.arange(device_total)[:, None]
+        wave = (np.arange(low, top)[None, :] * device_total + device).reshape(-1, 1)
+        phase = 2.0 * math.pi * ((wave * longitude) % lon_count) / lon_count
+        active = (wave <= TRUNC) / math.sqrt(lon_count)
+        parts += [np.cos(phase) * active, -np.sin(phase) * active]
+    return np.concatenate(parts).astype(np.float32).astype(jnp.bfloat16)
 
 
 def start_table(device_total, slots, slot_rows):
@@ -105,7 +108,6 @@
 ):
     lat_devices, tm_devices, rows, months, lon_count, slots, slot_rows, depth = dims
     device_total = lat_devices * tm_devices
-    groups = device_total // GROUP
     share = HALF // months
     high = rows // share
     lat_total = lat_devices * rows
@@ -118,35 +120,38 @@
     tm_me = lax.axis_index("tm")
     me = lat_me * tm_devices + tm_me
 
-    def coords(device):
-        return (device // tm_devices, lax.rem(device, tm_devices))
+    phases = phase_bounds(slots)
+
+    def each_peer(act):
+        def row(lat):
+            for tm in range(tm_devices):
+                act(lat, tm)
+
+        pl.loop(lat_me + 1, lat_devices)(row)
+        pl.loop(0, lat_me)(row)
+        for tm in range(tm_devices):
+
+            @pl.when(tm_me != tm)
+            def _():
+                act(lat_me, tm)
 
     x_copy = pltpu.make_async_copy(x_hbm, x_ref, x_sem)
     x_copy.start()
 
-    def table_copy(group):
-        return pltpu.make_async_copy(
-            table_hbm.at[group], table_ref.at[group], table_sem.at[group]
-        )
-
-    @pl.loop(0, groups)
-    def _(group):
-        table_copy(group).start()
+    def table_copy(phase):
+        low, top = phases[phase]
+        span = pl.ds(2 * device_total * low, 2 * device_total * (top - low))
+        return pltpu.make_async_copy(table_hbm.at[span], table_ref.at[span], table_sem.at[phase])
+
+    for phase in range(len(phases)):
+        table_copy(phase).start()
 
     barrier = pltpu.get_barrier_semaphore()
-
-    @pl.loop(1, device_total)
-    def _(step):
-        pl.semaphore_signal(
-            barrier,
-            inc=1,
-            device_id=coords(lax.rem(me + step, device_total)),
-            device_id_type=MESH,
-        )
-
-    group_rows = GROUP * slots
-    lane = lax.broadcasted_iota(jnp.int32, (group_rows, LANES), 1)
-    lower = lane < HALF
+    each_peer(
+        lambda lat, tm: pl.semaphore_signal(
+            barrier, inc=1, device_id=(lat, tm), device_id_type=MESH
+        )
+    )
 
     for first, last, count in runs:
         if count < slots:
@@ -155,13 +160,13 @@
             def _(source):
                 inbox[source, count:] = jnp.zeros((slots - count, high, LANES), jnp.bfloat16)
 
-    x_copy.wait()
-
-    @pl.loop(0, groups)
-    def _(group):
-        table_copy(group).wait()
+    def transform(phase):
+        low, top = phases[phase]
+        group_rows = device_total * (top - low)
+        lower = lax.broadcasted_iota(jnp.int32, (group_rows, LANES), 1) < HALF
+        table_copy(phase).wait()
         values = lax.dot_general(
-            table_ref[group],
+            table_ref[2 * device_total * low : 2 * device_total * top],
             x_ref[...],
             (((1,), (1,)), ((), ())),
             preferred_element_type=jnp.float32,
@@ -173,38 +178,36 @@
             odd = jnp.where(lower, pltpu.roll(cosine, HALF, 1), sine)
             spread[pl.ds(2 * block, group_rows, stride=high), :] = even
             spread[pl.ds(2 * block + 1, group_rows, stride=high), :] = odd
-        packed = spread[...].astype(jnp.bfloat16)
-        outbox[pl.ds(group * GROUP, GROUP)] = packed.reshape(GROUP, slots, high, LANES)
-
-    pl.semaphore_wait(barrier, device_total - 1)
-
-    phase_length = -(-slots // PHASES)
-    phases = [(low, min(low + phase_length, slots)) for low in range(0, slots, phase_length)]
-
-    def exchange(phase, count, target, source):
+        packed = spread[: group_rows * high].astype(jnp.bfloat16)
+        outbox[:, low:top] = packed.reshape(device_total, top - low, high, LANES)
+
+    def exchange(phase, count, lat, tm, source):
         low, top = phases[phase]
         span = pl.ds(low, min(count, top) - low)
+        target = lat * tm_devices + tm
         return pltpu.make_async_remote_copy(
             src_ref=outbox.at[target, span],
             dst_ref=inbox.at[source, span],
             send_sem=send_sem.at[phase, target],
             recv_sem=recv_sem.at[phase, source],
-            device_id=coords(target),
+            device_id=(lat, tm),
             device_id_type=MESH,
         )
 
-    def each_send(act):
-        for phase in range(len(phases)):
-            for first, last, count in runs:
-                if count > phases[phase][0]:
-
-                    @pl.when((lat_me >= first) & (lat_me < last))
-                    def _():
-                        @pl.loop(1, device_total)
-                        def _(step):
-                            act(exchange(phase, count, lax.rem(me + step, device_total), me))
-
-    each_send(lambda copy: copy.start())
+    def each_send(phase, act):
+        for first, last, count in runs:
+            if count > phases[phase][0]:
+
+                @pl.when((lat_me >= first) & (lat_me < last))
+                def _():
+                    each_peer(lambda lat, tm: act(exchange(phase, count, lat, tm, me)))
+
+    x_copy.wait()
+    for phase in range(len(phases)):
+        transform(phase)
+        if phase == 0:
+            pl.semaphore_wait(barrier, device_total - 1)
+        each_send(phase, lambda copy: copy.start())
 
     inbox[me] = outbox[me]
 
@@ -310,11 +313,14 @@
         for first, last, count in runs:
             if count > low:
 
-                @pl.loop(first * tm_devices, last * tm_devices)
-                def _(source):
-                    @pl.when(source != me)
-                    def _():
-                        exchange(phase, count, source, source).wait_recv()
+                @pl.loop(first, last)
+                def _(lat):
+                    for tm in range(tm_devices):
+                        source = lat * tm_devices + tm
+
+                        @pl.when(source != me)
+                        def _():
+                            exchange(phase, count, lat, tm, source).wait_recv()
 
         pl.loop(low, top)(add_slot)
 
@@ -337,8 +343,11 @@
         gram = block if gram is None else gram + block
     local_gram[...] = gram.reshape(pieces, PIECE, month_total)
 
+    lat_step = stride // tm_devices
+    first_lat = first_owner // tm_devices
+
     def owner(piece):
-        return first_owner + piece * stride
+        return first_lat + piece * lat_step
 
     def send_part(piece, source):
         return pltpu.make_async_remote_copy(
@@ -346,60 +355,48 @@
             dst_ref=parts.at[source],
             send_sem=part_send.at[piece],
             recv_sem=part_recv.at[source],
-            device_id=coords(owner(piece)),
+            device_id=(owner(piece), 0),
             device_id_type=MESH,
         )
 
-    def send_sum(piece, target):
+    def send_sum(piece, lat, tm):
         return pltpu.make_async_remote_copy(
             src_ref=own_sum,
             dst_ref=full.at[piece],
-            send_sem=sum_send.at[target],
+            send_sem=sum_send.at[lat * tm_devices + tm],
             recv_sem=sum_recv.at[piece],
-            device_id=coords(target),
+            device_id=(lat, tm),
             device_id_type=MESH,
         )
+
+    def not_mine(piece):
+        return (owner(piece) != lat_me) | (tm_me != 0)
 
     @pl.loop(0, pieces)
     def _(piece):
-        @pl.when(owner(piece) != me)
+        @pl.when(not_mine(piece))
         def _():
             send_part(piece, me).start()
 
-    is_owner = (
-        (me >= first_owner)
-        & (me < first_owner + pieces * stride)
-        & (lax.rem(me - first_owner + device_total, stride) == 0)
-    )
-    my_piece = lax.rem(me - first_owner + device_total, device_total) // stride
-
-    @pl.when(is_owner)
-    def _():
-        parts[me] = local_gram[my_piece]
-
-        @pl.loop(1, device_total)
-        def _(step):
-            source = lax.rem(me + step, device_total)
-            send_part(my_piece, source).wait_recv()
-
-        total = lax.fori_loop(
-            0,
-            device_total,
-            lambda source, value: value + parts[source],
-            jnp.zeros((PIECE, month_total), jnp.float32),
-        )
-        own_sum[...] = total
-        full[my_piece] = total
-
-        @pl.loop(1, device_total)
-        def _(step):
-            send_sum(my_piece, lax.rem(me + step, device_total)).start()
+    for phase in range(len(phases)):
+        each_send(phase, lambda copy: copy.wait_send())
 
     @pl.loop(0, pieces)
     def _(piece):
-        @pl.when(owner(piece) != me)
+        @pl.when((owner(piece) == lat_me) & (tm_me == 0))
         def _():
-            send_sum(piece, me).wait_recv()
+            parts[me] = local_gram[piece]
+            each_peer(lambda lat, tm: send_part(piece, lat * tm_devices + tm).wait_recv())
+            total = jnp.sum(parts[...], axis=0)
+            own_sum[...] = total
+            full[piece] = total
+            each_peer(lambda lat, tm: send_sum(piece, lat, tm).start())
+
+    @pl.loop(0, pieces)
+    def _(piece):
+        @pl.when(not_mine(piece))
+        def _():
+            send_sum(piece, lat_me, tm_me).wait_recv()
 
     gram = full[...].reshape(month_total, month_total)
     on_diagonal = lax.broadcasted_iota(jnp.int32, gram.shape, 0) == lax.broadcasted_iota(
@@ -409,19 +406,15 @@
     mine = full[pl.ds(tm_me * (months // PIECE), months // PIECE)].reshape(months, month_total)
     out_ref[...] = month_total * mine / (trace + 1e-06)
 
-    each_send(lambda copy: copy.wait_send())
-
     @pl.loop(0, pieces)
     def _(piece):
-        @pl.when(owner(piece) != me)
+        @pl.when(not_mine(piece))
         def _():
             send_part(piece, me).wait_send()
 
-    @pl.when(is_owner)
-    def _():
-        @pl.loop(1, device_total)
-        def _(step):
-            send_sum(my_piece, lax.rem(me + step, device_total)).wait_send()
+        @pl.when((owner(piece) == lat_me) & (tm_me == 0))
+        def _():
+            each_peer(lambda lat, tm: send_sum(piece, lat, tm).wait_send())
 
 
 def solution(mesh):
@@ -445,7 +438,8 @@
         starts = jnp.asarray(start_table(device_total, slots, slot_rows))
         lats = jnp.asarray(lat_table(lat_total, share))
         runs = needed_slots(lat_devices, device_total, slots, rows)
-        phases = -(-slots // -(-slots // PHASES))
+        phases = phase_bounds(slots)
+        longest = max(top - low for low, top in phases)
         hbm = pl.BlockSpec(memory_space=pl.ANY)
         vmem = pl.BlockSpec(memory_space=pltpu.VMEM)
         dma = pltpu.SemaphoreType.DMA
@@ -457,7 +451,7 @@
             scratch_shapes=[
                 pltpu.VMEM((rows * months, lon_count), jnp.bfloat16),
                 pltpu.VMEM(table.shape, jnp.bfloat16),
-                pltpu.VMEM((GROUP * slots * high, LANES), jnp.float32),
+                pltpu.VMEM((device_total * longest * high, LANES), jnp.float32),
                 pltpu.VMEM((device_total, slots, high, LANES), jnp.bfloat16),
                 pltpu.VMEM((device_total, slots, high, LANES), jnp.bfloat16),
                 pltpu.VMEM((lat_total // LANES, slot_rows * depth, LANES), jnp.float32),
@@ -467,9 +461,9 @@
                 pltpu.VMEM((PIECE, month_total), jnp.float32),
                 pltpu.VMEM((pieces, PIECE, month_total), jnp.float32),
                 dma,
-                dma((table.shape[0],)),
-                dma((phases, device_total)),
-                dma((phases, device_total)),
+                dma((len(phases),)),
+                dma((len(phases), device_total)),
+                dma((len(phases), device_total)),
                 dma((pieces,)),
                 dma((device_total,)),
                 dma((device_total,)),

time: 50 us -> 47.3 us (0.946)
  Pallas kernels: 48.4 us -> 45.8 us
    pallas_call x1, Pallas kernels: 48.4 us -> 45.8 us  [local(): pl.pallas_call(functools.partial(kernel, dims, runs), out_shape=jax.Shape...]
where the time goes in v3:
time: 47.3 us; the launch traced here: 47.1 us
  Pallas kernels  45.8 us (97%)
  local copies, waits for them, and re-layouts  1.32 us (3%)
    pallas_call x1, Pallas kernels, local(): pl.pallas_call(functools.partial(kernel, dims, runs), out_shape=jax.Shape...  45.8 us
    unnamed x1, local copies, waits for them, and re-layouts  1.32 us

profile of v3, /device:TPU:0, one launch (start us, length us, event | category | flops | bytes accessed | tf_op | source)
XLA Modules:
  0.0 47.1 jit_solution(10612153609692254009)
XLA Ops:
  0.0 45.8 %shard_map.46 = f32[32,64]{1,0:T(8,128)} custom-call(bf16[1024,1024]{1,0:T(8,128)(2,1)} %bitcast.1, bf16[704,1024]{1,0:T(8,128)(2,1)} %constant.6.clone.table_hbm, f32[32,16,128]{2,1,0:T(8,128)} %constant.7.clone.start_ref, f32[3,4,128]{2,1,0:T(4,128)} %constant.8.clone.lat_ref), custom_call_target="tpu_custom_call" | custom-call | tf_op jit(solution)/shard_map/pallas_call | solution.py:446
  45.8 1.3 %copy.6 = f32[32,64]{1,0:T(8,128)} copy(f32[32,64]{1,0:T(8,128)} %shard_map.46) | data formatting | bytes 16384

commit v4 on v3

--- a/solution.py
+++ b/solution.py
@@ -13,7 +13,7 @@
 LANES = 128
 HALF = 64
 PIECE = 8
-PHASES = 4
+PHASES = 3
 MESH = pl.DeviceIdType.MESH
 
 

time: 47.3 us -> 46.8 us (0.989)
  Pallas kernels: 45.8 us -> 45.2 us
    pallas_call x1, Pallas kernels: 45.8 us -> 45.2 us  [local(): pl.pallas_call(functools.partial(kernel, dims, runs), out_shape=jax.Shape...]
where the time goes in v4:
time: 46.8 us; the launch traced here: 46.6 us
  Pallas kernels  45.2 us (97%)
  local copies, waits for them, and re-layouts  1.32 us (3%)
    pallas_call x1, Pallas kernels, local(): pl.pallas_call(functools.partial(kernel, dims, runs), out_shape=jax.Shape...  45.2 us
    unnamed x1, local copies, waits for them, and re-layouts  1.32 us

profile of v4, /device:TPU:0, one launch (start us, length us, event | category | flops | bytes accessed | tf_op | source)
XLA Modules:
  0.0 46.6 jit_solution(2618711879356109698)
XLA Ops:
  0.0 45.2 %shard_map.46 = f32[32,64]{1,0:T(8,128)} custom-call(bf16[1024,1024]{1,0:T(8,128)(2,1)} %bitcast.1, bf16[704,1024]{1,0:T(8,128)(2,1)} %constant.6.clone.table_hbm, f32[32,16,128]{2,1,0:T(8,128)} %constant.7.clone.start_ref, f32[3,4,128]{2,1,0:T(4,128)} %constant.8.clone.lat_ref), custom_call_target="tpu_custom_call" | custom-call | tf_op jit(solution)/shard_map/pallas_call | solution.py:446
  45.3 1.3 %copy.6 = f32[32,64]{1,0:T(8,128)} copy(f32[32,64]{1,0:T(8,128)} %shard_map.46) | data formatting | bytes 16384
